TPU v7x, 256 devices: a whole 4x4x8 slice. The times are simulated.
256 devices in a mesh: clusters: 8 (over y, x_hi), members: 32 (over z, x_lo, core).
Axes of the slice: x: 4 (x_hi: 2, x_lo: 2; x = x_hi * 2 + x_lo), y: 4, z: 8, core: 2. Of those that a mesh axis runs over, the one named last changes fastest.
Arguments:
- embeddings: float32 [131072, 1024], P(('clusters', 'members')), parts along dimension 0, as said below
- member_order: int32 [131072], P(('clusters', 'members')), parts along dimension 0, may hold values from 0 to 16383, each once
- threshold: float32 [8], P('clusters'), parts along dimension 0, may hold values from 0.25 to 0.5
Outputs:
- best_similarity: float32 [131072], P(('clusters', 'members')), parts along dimension 0
- excess: float32 [131072], P(('clusters', 'members')), parts along dimension 0
There are 8 independent parts, one for each index of `clusters`. A program takes and returns all parts, laid end to end along the dimension named above; each array names one. Nothing has to cross between parts.
Inputs may be any that keep to these rules, and one draw needn't show every extreme that they name: member_order holds each of 0 to 16383 once. real-valued embeddings.
All inputs are finite; a program needn't handle non-finite values.
Results may differ from a plain program's by a relative error of at most 0.00051.
Values may be sent and summed in bfloat16 or wider, within the bound.
A program may use at most 128 MiB of HBM per device.

v0:
```python
import jax
import jax.numpy as jnp
from jax import lax
from jax.sharding import PartitionSpec as P


def block_scores(unit, other):
    return lax.dot_general(
        unit, other, (((1,), (1,)), ((), ())), preferred_element_type=jnp.float32
    )


def shards(embeddings, member_order, threshold):
    unit = (
        embeddings * lax.rsqrt(jnp.sum(embeddings * embeddings, axis=1, keepdims=True) + 1e-06)
    ).astype(jnp.bfloat16)
    floor_value = jnp.float32(-1.0)
    start_best = jnp.full((unit.shape[0],), -1.0, jnp.float32)
    scores = block_scores(unit, lax.all_gather(unit, "members", axis=0, tiled=True))
    mask = (
        lax.all_gather(member_order, "members", axis=0, tiled=True)[None, :] < member_order[:, None]
    )
    best = jnp.maximum(start_best, jnp.max(jnp.where(mask, scores, floor_value), axis=1))
    excess = jnp.maximum(best - threshold[0], jnp.float32(0.0))
    return (best, excess)


def solution(mesh):
    placed = (P(("clusters", "members"), None), P(("clusters", "members")), P("clusters"))
    return jax.shard_map(
        shards,
        mesh=mesh,
        in_specs=placed,
        out_specs=(P(("clusters", "members")), P(("clusters", "members"))),
        check_vma=False,
    )
```

profile of v0, /device:TPU:1, one launch (start us, length us, event | category | flops | bytes accessed | tf_op | source)
XLA Modules:
  0.0 231.1 jit_solution(13599985710889065328)
XLA Ops:
  7.2 0.0 all-gather.3.cloned.1.call-start
  7.2 1.8 multiply_reduce_fusion
  9.0 2.8 %multiply_convert_fusion = bf16[512,1024]{1,0:T(8,128)(2,1)} fusion(f32[512,1024]{1,0:T(8,128)} %param.3, f32[512]{0:T(512)S(1)} %add_rsqrt_fusion), kind=kLoop, calls=%fused_computation.1 | loop fusion | flops 1048576 | bytes 3147776 | tf_op jit(solution)/shard_map/convert_element_type | solution.py:16
  11.8 0.0 all-gather.3.cloned.1.call-update
  12.5 39.5 %all-gather = s32[32,1,512]{2,1,0:T(1,128)S(1)} all-gather(s32[1,1,512]{2,1,0:T(1,128)} %bitcast.7), channel_id=1, replica_groups=mesh['clusters'=8,'members'=32] {'members'}, dimensions={0}, use_global_device_ids=true | all-gather | bytes 67584 | tf_op jit(solution)/shard_map/all_gather | solution.py:21
  51.9 148.5 %all-gather.3.cloned.1.call-done = bf16[16384,1024]{1,0:T(8,128)(2,1)} async-done(((bf16[512,1024]{1,0:T(8,128)(2,1)}), bf16[16384,1024]{1,0:T(8,128)(2,1)}) %all-gather.3.cloned.1.call-update) | async-done | bytes 33554448 | tf_op jit(solution)/shard_map/all_gather | solution.py:19
  200.5 23.2 %select_reduce_fusion = f32[512]{0:T(512)S(1)} fusion(bf16[512,1024]{1,0:T(8,128)(2,1)} %multiply_convert_fusion, bf16[16384,1024]{1,0:T(8,128)(2,1)} %all-gather.3.cloned.1.call-done, s32[16384]{0:T(1024)S(1)} %bitcast.6, s32[512]{0:T(512)} %param.4), kind=kOutput, calls=%fused_computation | convolution fusion | flops 17205035008 | bytes 34672640 | tf_op jit(solution)/shard_map/dot_general | solution.py:8
  223.7 0.6 subtract_maximum_fusion
  (1 shorter events, 0.0 us)
Async XLA Ops:
  7.2 193.3 %all-gather.3.cloned.1.call-start = ((), (), s32[]{:S(2)}) async-start(), calls=%async_computation | async-start | bytes 34603008 | tf_op jit(solution)/shard_map/all_gather | solution.py:19
Sparse Core Ops, SparseCore 0:
  11.9 188.4 all-gather.2
where the time goes:
time: 231 us
  waiting for transfers between devices  149 us (65%)
  blocking collectives  39.5 us (17%)
  matrix products  23.2 us (10%)
  between operations  14.7 us (6%)
  other arithmetic  5.16 us (2%)
    all_gather x1, waiting for transfers between devices, shards(): lax.all_gather(unit, 'members', axis=0, tiled=True)  149 us
    all_gather x1, blocking collectives, shards(): lax.all_gather(member_order, 'members', axis=0, tiled=True)[None, :]  39.5 us
    dot_general x1, matrix products, block_scores(): lax.dot_general(unit, other, (((1,), (1,)), ((), ())), preferred_element_...  23.2 us
  transfers between devices with their start and end apart: 1, of which 1 were waited for; matrix products, arithmetic and copies ran while one was open for 0% of the time, Pallas kernels for 0%

commit v1 on v0

--- a/solution.py
+++ b/solution.py
@@ -2,6 +2,13 @@
 import jax.numpy as jnp
 from jax import lax
 from jax.sharding import PartitionSpec as P
+
+direct_the_spot = lambda buf, lane_axis: jnp.concatenate(
+    lax.all_to_all(
+        jnp.stack([buf] * lax.psum(1, lane_axis), axis=0), lane_axis, split_axis=0, concat_axis=0
+    ),
+    axis=0,
+)
 
 
 def block_scores(unit, other):
@@ -17,9 +24,7 @@
     floor_value = jnp.float32(-1.0)
     start_best = jnp.full((unit.shape[0],), -1.0, jnp.float32)
     scores = block_scores(unit, lax.all_gather(unit, "members", axis=0, tiled=True))
-    mask = (
-        lax.all_gather(member_order, "members", axis=0, tiled=True)[None, :] < member_order[:, None]
-    )
+    mask = direct_the_spot(member_order, "members")[None, :] < member_order[:, None]
     best = jnp.maximum(start_best, jnp.max(jnp.where(mask, scores, floor_value), axis=1))
     excess = jnp.maximum(best - threshold[0], jnp.float32(0.0))
     return (best, excess)

time: 231 us -> 231 us (level)
  blocking collectives: 39.5 us -> 0 us
  waiting for transfers between devices: 149 us -> 176 us
  starting transfers between devices: 0.04 us -> 11.1 us
    all_gather x1 -> x0, blocking collectives: 39.5 us -> none  [shards(): lax.all_gather(member_order, 'members', axis=0, tiled=True)[None, :]]
    all_gather x1, waiting for transfers between devices: 149 us -> 168 us  [shards(): lax.all_gather(unit, 'members', axis=0, tiled=True)]
    all_to_all x0 -> x1, starting transfers between devices: none -> 11 us  [lax.all_to_all(jnp.stack([buf] * lax.psum(1, lane_axis), axis=0), lane_ax...]
    all_to_all x0 -> x1, waiting for transfers between devices: none -> 7.62 us  [lax.all_to_all(jnp.stack([buf] * lax.psum(1, lane_axis), axis=0), lane_ax...]
  transfers between devices with their start and end apart: 1 -> 2, of which waited for: 1 -> 2; matrix products, arithmetic and copies ran while one was open for 0% -> 1% of each run, Pallas kernels for 0% -> 0%
where the time goes in v1:
time: 231 us
  waiting for transfers between devices  176 us (76%)
  matrix products  23.2 us (10%)
  between operations  14.7 us (6%)
  starting transfers between devices  11.1 us (5%)
  other arithmetic  5.16 us (2%)
    all_gather x1, waiting for transfers between devices, shards(): lax.all_gather(unit, 'members', axis=0, tiled=True)  168 us
    dot_general x1, matrix products, block_scores(): lax.dot_general(unit, other, (((1,), (1,)), ((), ())), preferred_element_...  23.2 us
    all_to_all x1, starting transfers between devices, lax.all_to_all(jnp.stack([buf] * lax.psum(1, lane_axis), axis=0), lane_ax...  11 us
    all_to_all x1, waiting for transfers between devices, lax.all_to_all(jnp.stack([buf] * lax.psum(1, lane_axis), axis=0), lane_ax...  7.62 us
  transfers between devices with their start and end apart: 2, of which 2 were waited for; matrix products, arithmetic and copies ran while one was open for 1% of the time, Pallas kernels for 0%

profile of v1, /device:TPU:1, one launch (start us, length us, event | category | flops | bytes accessed | tf_op | source)
XLA Modules:
  0.0 231.1 jit_solution(8264312339589648375)
XLA Ops:
  7.2 0.0 all-gather.2.cloned.1.call-start
  7.2 1.8 multiply_reduce_fusion
  9.0 2.8 %multiply_convert_fusion = bf16[512,1024]{1,0:T(8,128)(2,1)} fusion(f32[512,1024]{1,0:T(8,128)} %param.3, f32[512]{0:T(512)S(1)} %add_rsqrt_fusion), kind=kLoop, calls=%fused_computation.1 | loop fusion | flops 1048576 | bytes 3147776 | tf_op jit(solution)/shard_map/convert_element_type | solution.py:23
  11.8 0.0 all-gather.2.cloned.1.call-update
  11.8 1.3 stack.2
  13.1 11.0 %all-to-all-start = ((s32[32,1,512]{2,1,0:T(1,128)}), s32[32,1,512]{2,1,0:T(1,128)S(1)}, u32[]{:S(2)}, u32[]{:S(2)}) async-start(s32[32,1,512]{2,1,0:T(1,128)} %stack.2), calls=%async_computation | async-start | bytes 131072 | tf_op jit(solution)/shard_map/all_to_all | solution.py:7
  24.8 7.6 %all-to-all-done = s32[32,1,512]{2,1,0:T(1,128)S(1)} async-done(((s32[32,1,512]{2,1,0:T(1,128)}), s32[32,1,512]{2,1,0:T(1,128)S(1)}, u32[]{:S(2)}, u32[]{:S(2)}) %all-to-all-start) | async-done | bytes 65568 | tf_op jit(solution)/shard_map/all_to_all | solution.py:7
  32.4 168.0 %all-gather.2.cloned.1.call-done = bf16[16384,1024]{1,0:T(8,128)(2,1)} async-done(((bf16[512,1024]{1,0:T(8,128)(2,1)}), bf16[16384,1024]{1,0:T(8,128)(2,1)}) %all-gather.2.cloned.1.call-update) | async-done | bytes 33554448 | tf_op jit(solution)/shard_map/all_gather | solution.py:26
  200.4 23.2 %select_reduce_fusion = f32[512]{0:T(512)S(1)} fusion(bf16[512,1024]{1,0:T(8,128)(2,1)} %multiply_convert_fusion, bf16[16384,1024]{1,0:T(8,128)(2,1)} %all-gather.2.cloned.1.call-done, s32[16384]{0:T(1024)S(1)} %bitcast.5, s32[512]{0:T(512)} %param.4), kind=kOutput, calls=%fused_computation | convolution fusion | flops 17205035008 | bytes 34672640 | tf_op jit(solution)/shard_map/dot_general | solution.py:15
  223.6 0.6 subtract_maximum_fusion
  (1 shorter events, 0.0 us)
Async XLA Ops:
  7.2 193.2 %all-gather.2.cloned.1.call-start = ((), (), s32[]{:S(2)}) async-start(), calls=%async_computation.1 | async-start | bytes 34603008 | tf_op jit(solution)/shard_map/all_gather | solution.py:26
  13.1 19.3 %all-to-all-start = ((s32[32,1,512]{2,1,0:T(1,128)}), s32[32,1,512]{2,1,0:T(1,128)S(1)}, u32[]{:S(2)}, u32[]{:S(2)}) async-start(s32[32,1,512]{2,1,0:T(1,128)} %stack.2), calls=%async_computation | async-start | bytes 131072 | tf_op jit(solution)/shard_map/all_to_all | solution.py:7
Sparse Core Ops, SparseCore 0:
  11.9 188.4 all-gather.1
